TPU v7x, 32 devices: a whole 2x2x4 slice. The times are simulated.
32 devices in a mesh: row: 8 (over z, y), col: 4 (over x, core).
Axes of the slice: x: 2, y: 2, z: 4, core: 2. Of those that a mesh axis runs over, the one named last changes fastest.
Arguments:
- grads: float32 [64, 20, 3, 4096], P(None, None, None, ('row', 'col')), may hold values from -6 to 6
- weights: float32 [64, 4096], P(None, ('row', 'col')), may hold values from 0.005 to 0.05
- counts: int32 [4096], P(('row', 'col')), may hold values from 1 to 8
- lame_first: float32 [4096], P(('row', 'col')), may hold values from 0.5 to 2
- shear: float32 [4096], P(('row', 'col')), may hold values from 0.5 to 2
- dest_owner: int32 [4096, 1], P(('row', 'col')), may hold values from 0 to 31; in each aligned block of 128 rows (0 to 127, 128 to 255, ...) at most 8 rows name the same one
- dest_slot: int32 [4096], P(('row', 'col')), may hold values from 0 to 127
Outputs:
- assembled: float32 [60, 60, 4096], P(None, None, ('row', 'col'))
Inputs may be any that keep to these rules, and one draw needn't show every extreme that they name: `dest_owner`: among the elements of one device, at most 8 have the same owner; in some device exactly 8 do.
All inputs are finite; a program needn't handle non-finite values.
Results may differ from a plain program's by a relative error of at most 0.0001.
Values sent between devices are 32-bit elements; how exact they have to be, the bound alone decides.
No kernel may reach another device: no remote copies, remote signals or barrier semaphores. Data moves between devices by JAX's collectives and lax.ppermute only.
A program may use at most 64 MiB of HBM per device.

v0:
```python
import jax
import jax.numpy as jnp
import numpy as np
from jax import lax
from jax.sharding import PartitionSpec as P

NF = 20
NDOF = 60
GP = 8
Q = 64
SLOTS_DEV = 128


def stiffness(gflat, weff, lame_first, shear):
    count = gflat.shape[2]
    moment = jnp.einsum(
        "qme,qne->mne", gflat * weff[:, None, :], gflat, precision=lax.Precision.HIGHEST
    )
    blocks = moment.reshape(NF, 3, NF, 3, count)
    across = jnp.einsum("akbke->abe", blocks)
    eye = jnp.eye(3, dtype=jnp.float32)
    result = lame_first * blocks + shear * (
        eye[None, :, None, :, None] * across[:, None, :, None, :]
        + jnp.transpose(blocks, (0, 3, 2, 1, 4))
    )
    return result.reshape(NDOF * NDOF, count)


def triangle_tables(order):
    upper_rows, upper_cols = np.triu_indices(order)
    lookup = np.zeros((order, order), np.int32)
    lookup[upper_rows, upper_cols] = np.arange(upper_rows.shape[0], dtype=np.int32)
    lookup[upper_cols, upper_rows] = np.arange(upper_rows.shape[0], dtype=np.int32)
    upper_index = (upper_rows * order + upper_cols).astype(np.int32)
    return (upper_index, lookup.reshape(order * order))


def deliver(payload, slotcol):
    return (
        lax.all_to_all(payload, ("row", "col"), split_axis=1, concat_axis=1, tiled=True),
        lax.all_to_all(slotcol, ("row", "col"), split_axis=1, concat_axis=1, tiled=True),
    )


def shards(grads, weights, counts, lame_first, shear, dest_owner, dest_slot):
    count = grads.shape[3]
    nrow = lax.axis_size("row")
    ncol = lax.axis_size("col")
    ndevices = nrow * ncol
    capacity = max(2, 2 * count // ndevices)
    width = ndevices * capacity
    points = lax.broadcasted_iota(jnp.int32, weights.shape, 0)
    weff = jnp.where(points < counts[None, :] * GP, weights, jnp.float32(0.0))
    squares = jnp.sum(grads * grads, axis=(1, 2))
    local_trace = jnp.sum((lame_first + 4.0 * shear) * jnp.sum(weff * squares, axis=0))
    total = lax.psum(local_trace, ("row", "col"))
    scale = total / (NDOF * count * ndevices)
    owner = dest_owner[:, 0]
    onehot = (owner[:, None] == lax.broadcasted_iota(jnp.int32, (count, ndevices), 1)).astype(
        jnp.int32
    )
    ranking = jnp.sum(jnp.cumsum(onehot, axis=0) * onehot, axis=1) - 1
    position = owner * capacity + ranking
    slotcol = (
        jnp.full((1, width), -1.0, jnp.float32).at[0, position].set(dest_slot.astype(jnp.float32))
    )
    gflat = grads.reshape(Q, NDOF, count)
    upper_index, mirror_index = triangle_tables(NDOF)
    local_blocks = stiffness(gflat, weff, lame_first, shear)
    upper_part = jnp.take(local_blocks, jnp.asarray(upper_index, jnp.int32), axis=0)
    payload = jnp.zeros((upper_part.shape[0], width), jnp.float32).at[:, position].set(upper_part)
    moved, slots_in = deliver(payload, slotcol)
    received = jnp.take(moved, jnp.asarray(mirror_index, jnp.int32), axis=0)
    slot_ids = slots_in[0].astype(jnp.int32)
    placing = (slot_ids[:, None] == lax.broadcasted_iota(jnp.int32, (width, SLOTS_DEV), 1)).astype(
        jnp.float32
    )
    summed = jnp.dot(
        received, placing, precision=lax.Precision.HIGHEST, preferred_element_type=jnp.float32
    )
    return (summed / scale).reshape(NDOF, NDOF, SLOTS_DEV)


def solution(mesh):
    in_specs = (
        P(None, None, None, ("row", "col")),
        P(None, ("row", "col")),
        P(("row", "col")),
        P(("row", "col")),
        P(("row", "col")),
        P(("row", "col"), None),
        P(("row", "col")),
    )
    out_specs = P(None, None, ("row", "col"))
    return jax.shard_map(shards, mesh=mesh, in_specs=in_specs, out_specs=out_specs, check_vma=False)
```

profile of v0, /device:TPU:0, one launch (start us, length us, event | category | flops | bytes accessed | tf_op | source)
XLA Modules:
  0.0 143.4 jit_solution(12971024460196947275)
XLA Ops:
  0.0 0.9 fusion.11
  0.9 0.2 reduce_window_sum.11
  1.1 0.8 select_reduce_fusion.1
  1.9 0.7 fusion.14
  2.6 0.7 convert_element_type.26
  3.2 1.0 scatter_custom_fusion.1
  4.2 0.7 all_to_all.17
  4.9 7.3 %all-to-all-start.1 = ((f32[1,32,8]{2,0,1:T(1,128)}), f32[1,32,8]{2,0,1:T(1,128)S(1)}, u32[]{:S(2)}, u32[]{:S(2)}) async-start(f32[1,32,8]{2,0,1:T(1,128)} %bitcast.9), calls=%async_computation.1 | async-start | bytes 32768 | tf_op jit(solution)/shard_map/all_to_all | solution.py:41
  12.3 1.7 %multiply_reduce_fusion = f32[64,128]{1,0:T(8,128)S(1)} fusion(f32[64,20,3,128]{3,0,2,1:T(8,128)} %param.9), kind=kLoop, calls=%fused_computation.14 | loop fusion | flops 974848 | bytes 1998848 | tf_op jit(solution)/shard_map/reduce_sum | solution.py:54
  14.0 0.1 copy.34
  14.1 4.7 %copy.35 = f32[64,60,128]{0,1,2:T(8,128)} copy(f32[64,60,128]{2,0,1:T(8,128)S(1)} %bitcast.22) | data formatting | bytes 3932160 | tf_op jit(solution)/shard_map/reshape | solution.py:67
  18.8 12.3 %fusion.4 = f32[60,60,128]{1,0,2:T(8,128)} fusion(f32[64,60,128]{0,1,2:T(8,128)} %copy.35, f32[64,128]{0,1:T(8,128)S(1)} %copy.34), kind=kOutput, calls=%fused_computation.12 | convolution fusion | flops 354385920 | bytes 3842048 | tf_op jit(solution)/shard_map/qme,qne->mne/dot_general | solution.py:16
  31.1 4.7 %copy.37 = f32[60,60,128]{2,1,0:T(8,128)} copy(f32[60,60,128]{1,0,2:T(8,128)} %fusion.4) | data formatting | bytes 3686400 | tf_op jit(solution)/shard_map/qme,qne->mne/transpose | solution.py:16
  35.9 3.0 %reshape.57 = f32[20,3,20,3,128]{4,3,2,1,0:T(4,128)S(1)} reshape(f32[60,60,128]{2,1,0:T(8,128)} %copy.37) | data formatting | bytes 3686400 | tf_op jit(solution)/shard_map/reshape | solution.py:19
  38.9 0.9 select_reduce_fusion
  39.8 0.5 fusion.3
  40.3 0.2 copy-done.4
  40.5 2.1 %copy.40 = f32[20,3,20,3,128]{4,3,2,1,0:T(4,128)} copy(f32[20,3,20,3,128]{4,2,3,1,0:T(8,128)S(1)} %fusion.3) | data formatting | bytes 3686400 | tf_op jit(solution)/shard_map/add | solution.py:22
  42.6 2.9 %reshape.58 = f32[3600,128]{1,0:T(8,128)S(1)} reshape(f32[20,3,20,3,128]{4,3,2,1,0:T(4,128)} %copy.40) | data formatting | bytes 3686400 | tf_op jit(solution)/shard_map/reshape | solution.py:26
  45.5 3.4 %gather_fusion = f32[1830,128]{1,0:T(8,128)S(1)} fusion(f32[3600,128]{1,0:T(8,128)S(1)} %reshape.58, s32[2048]{0:T(1024)S(1)} %pad_clamp_fusion.1), kind=kCustom, calls=%fused_computation | custom fusion | bytes 1881240 | tf_op jit(solution)/shard_map/jit(_take)/gather | solution.py:70
  48.9 0.3 copy.41
  49.3 2.5 %scatter_custom_fusion = f32[1830,256]{0,1:T(8,128)} fusion(s32[128]{0:T(128)S(1)} %fusion.14, f32[128,1830]{1,0:T(8,128)S(1)} %copy.41, f32[]{:T(128)} %constant.29.clone.1), kind=kCustom, calls=%fused_computation.15 | custom fusion | bytes 1873924 | tf_op jit(solution)/shard_map/scatter | solution.py:71
  51.8 5.8 %all-to-all-start = ((f32[1830,32,8]{0,2,1:T(8,128)}), f32[1830,32,8]{0,2,1:T(8,128)S(1)}, u32[]{:S(2)}, u32[]{:S(2)}) async-start(f32[1830,32,8]{0,2,1:T(8,128)} %bitcast.7), calls=%async_computation | async-start | bytes 3932160 | tf_op jit(solution)/shard_map/all_to_all | solution.py:40
  57.7 0.7 multiply_reduce_fusion.2
  58.3 65.9 %psum.7 = f32[]{:T(128)} all-reduce(f32[]{:T(128)} %multiply_reduce_fusion.2), channel_id=1, replica_groups=mesh['row'=8,'col'=4] {'row','col'}, use_global_device_ids=true, to_apply=%region_8.9 | all-reduce | flops 1 | bytes 8 | tf_op jit(solution)/shard_map/psum | solution.py:56
  124.9 0.1 convert_reduce_fusion
  125.0 0.1 convert_element_type.28
  125.1 1.3 copy-done.1
  126.4 1.8 %copy.42 = f32[1830,256]{1,0:T(8,128)S(1)} copy(f32[1830,256]{0,1:T(8,128)} %bitcast.23) | data formatting | bytes 3747840 | tf_op jit(solution)/shard_map/all_to_all | solution.py:40
  128.2 10.0 %gather_fusion.1 = f32[3600,256]{1,0:T(8,128)} fusion(f32[1830,256]{1,0:T(8,128)S(1)} %copy.42, s32[4096]{0:T(1024)S(1)} %pad_clamp_fusion), kind=kCustom, calls=%fused_computation.1 | custom fusion | bytes 7387200 | tf_op jit(solution)/shard_map/jit(_take)/gather | solution.py:73
  138.2 3.9 %convolution_divide_fusion = f32[3600,128]{1,0:T(8,128)S(1)} fusion(f32[3600,256]{1,0:T(8,128)} %gather_fusion.1, f32[]{:T(128)S(6)} %div.9, s32[256]{0:T(256)S(1)} %convert_element_type.28), kind=kOutput, calls=%fused_computation.6 | convolution fusion | flops 1416071168 | bytes 5530628 | tf_op jit(solution)/shard_map/dot_general | solution.py:78
  142.0 1.4 reshape.59
  (22 shorter events, 0.1 us)
Async XLA Ops:
  0.0 14.1 %copy-start = (f32[64,20,3,128]{3,0,2,1:T(8,128)S(1)}, f32[64,20,3,128]{3,0,2,1:T(8,128)}, u32[]{:S(2)}) copy-start(f32[64,20,3,128]{3,0,2,1:T(8,128)} %param.9) | copy-start | bytes 5898244
  0.0 14.0 %copy-start.7 = (s32[128]{0:T(128)S(1)}, s32[128]{0:T(128)}, u32[]{:S(2)}) copy-start(s32[128]{0:T(128)} %param.11) | copy-start | bytes 1540
  0.0 14.0 %copy-start.2 = (f32[64,128]{1,0:T(8,128)S(1)}, f32[64,128]{1,0:T(8,128)}, u32[]{:S(2)}) copy-start(f32[64,128]{1,0:T(8,128)} %param.10) | copy-start | bytes 98308
  4.9 46.9 %all-to-all-start.1 = ((f32[1,32,8]{2,0,1:T(1,128)}), f32[1,32,8]{2,0,1:T(1,128)S(1)}, u32[]{:S(2)}, u32[]{:S(2)}) async-start(f32[1,32,8]{2,0,1:T(1,128)} %bitcast.9), calls=%async_computation.1 | async-start | bytes 32768 | tf_op jit(solution)/shard_map/all_to_all | solution.py:41
  38.8 0.9 copy-start.5
  38.9 0.9 copy-start.6
  39.8 0.7 copy-start.4
  51.8 73.1 %copy-start.3 = (s32[3600]{0:T(1024)S(1)}, s32[3600]{0:T(1024)}, u32[]{:S(2)}) copy-start(s32[3600]{0:T(1024)} %constant.83) | copy-start | bytes 43204
  51.8 73.3 %all-to-all-start = ((f32[1830,32,8]{0,2,1:T(8,128)}), f32[1830,32,8]{0,2,1:T(8,128)S(1)}, u32[]{:S(2)}, u32[]{:S(2)}) async-start(f32[1830,32,8]{0,2,1:T(8,128)} %bitcast.7), calls=%async_computation | async-start | bytes 3932160 | tf_op jit(solution)/shard_map/all_to_all | solution.py:40
  125.1 1.3 copy-start.1
where the time goes:
time: 144 us; the launch traced here: 143 us
  blocking collectives  65.9 us (46%)
  local copies, waits for them, and re-layouts  40.2 us (28%)
  matrix products  16.2 us (11%)
  starting transfers between devices  13.2 us (9%)
  other arithmetic  7.07 us (5%)
    psum x1, blocking collectives, shards(): total = lax.psum(local_trace, ('row', 'col'))  65.9 us
    dot_general x1, matrix products, stiffness(): jnp.einsum('qme,qne->mne', gflat * weff[:, None, :], gflat, precision=lax...  12.3 us
    gather x1, local copies, waits for them, and re-layouts, shards(): received = jnp.take(moved, jnp.asarray(mirror_index, jnp.int32), axis=0)  9.98 us
    all_to_all x1, starting transfers between devices, deliver(): lax.all_to_all(slotcol, ('row', 'col'), split_axis=1, concat_axis=1, tile...  7.33 us
    all_to_all x1, starting transfers between devices, deliver(): lax.all_to_all(payload, ('row', 'col'), split_axis=1, concat_axis=1, tile...  5.83 us
    transpose x1, local copies, waits for them, and re-layouts, stiffness(): jnp.einsum('qme,qne->mne', gflat * weff[:, None, :], gflat, precision=lax...  4.73 us
    reshape x1, local copies, waits for them, and re-layouts, shards(): gflat = grads.reshape(Q, NDOF, count)  4.68 us
    dot_general x1, matrix products, shards(): jnp.dot(received, placing, precision=lax.Precision.HIGHEST, preferred_ele...  3.85 us
  transfers between devices with their start and end apart: 2, of which 0 were waited for; matrix products, arithmetic and copies ran while one was open for 28% of the time, Pallas kernels for 0%

commit v1 on v0

v1 whole, which is shorter than its diff:
```python
import functools

import jax
import jax.numpy as jnp
from jax import lax
from jax.experimental import pallas as pl
from jax.experimental.pallas import tpu as pltpu
from jax.sharding import PartitionSpec as P

NF = 20
NDOF = 60
GP = 8
SLOTS_DEV = 128
LANES = 128
AXES = ("row", "col")

PAIRS = NF * (NF - 1) // 2
PAIRS_UP = -(-PAIRS // 8) * 8
DIAG_UP = -(-NF // 8) * 8
DIAG_BASE = 9 * PAIRS_UP
UPPER = ((0, 0), (0, 1), (0, 2), (1, 1), (1, 2), (2, 2))
SLOT_WORD = DIAG_BASE + 6 * DIAG_UP
TRACE_WORD = SLOT_WORD + 1
WORDS = -(-(TRACE_WORD + 1) // LANES) * LANES


def split(value):
    high = value.astype(jnp.bfloat16)
    low = (value - high.astype(jnp.float32)).astype(jnp.bfloat16)
    return high, low


def pick(onehot, value, dims):
    high, low = split(value)
    dot = functools.partial(
        lax.dot_general, dimension_numbers=(dims, ((), ())), preferred_element_type=jnp.float32
    )
    return dot(onehot, high) + dot(onehot, low)


def fold(parts):
    row = lax.broadcasted_iota(jnp.int32, parts[0].shape, 0)
    for bit in (1, 2, 4):
        keep = (row & bit) == 0
        parts = [
            jnp.where(keep, first, second)
            + pltpu.roll(jnp.where(keep, second, first), 8 - bit, 0)
            for first, second in zip(parts[0::2], parts[1::2])
        ]
    return parts[0]


def element_kernel(
    ndevices,
    capacity,
    g_ref,
    w_ref,
    counts_ref,
    lame_ref,
    shear_ref,
    owner_ref,
    slot_ref,
    out_ref,
    wg_ref,
    k_ref,
):
    points, count = w_ref.shape
    width = ndevices * capacity
    qrow = lax.broadcasted_iota(jnp.int32, (points, count), 0)
    weff = jnp.where(qrow < counts_ref[...] * GP, w_ref[...], 0.0)

    def weigh(m, carry):
        wg_ref[m] = g_ref[m] * weff
        return carry

    lax.fori_loop(0, NDOF, weigh, 0, unroll=4)
    lam = jnp.broadcast_to(lame_ref[...], (8, count))
    mu = jnp.broadcast_to(shear_ref[...], (8, count))
    both = lam + mu

    def products(a, b, wanted):
        sums = {}
        for t in range(points // 8):
            rows = pl.ds(8 * t, 8)
            left = [wg_ref[3 * a + i, rows, :] for i in range(3)]
            right = [g_ref[3 * b + j, rows, :] for j in range(3)]
            for i, j in wanted:
                term = left[i] * right[j]
                sums[i, j] = term if t == 0 else sums[i, j] + term
        return sums

    full = tuple((i, j) for i in range(3) for j in range(3))

    def off_diagonal(group, carry):
        parts = []
        for k in range(8):
            p = group * 8 + k
            d = p // NF
            a = p - d * NF
            b = a + d + 1
            b = jnp.where(b >= NF, b - NF, b)
            parts.append(products(a, b, full))
        m = {ij: fold([part[ij] for part in parts]) for ij in full}
        across = mu * (m[0, 0] + m[1, 1] + m[2, 2])
        for i, j in full:
            value = both * m[i, i] + across if i == j else lam * m[i, j] + mu * m[j, i]
            start = pl.multiple_of((3 * i + j) * PAIRS_UP + group * 8, 8)
            k_ref[pl.ds(start, 8), :] = value
        return carry

    lax.fori_loop(0, PAIRS_UP // 8, off_diagonal, 0)

    row = lax.broadcasted_iota(jnp.int32, (8, count), 0)

    def diagonal(group, trace):
        parts = []
        for k in range(8):
            a = jnp.minimum(group * 8 + k, NF - 1)
            parts.append(products(a, a, UPPER))
        m = {ij: fold([part[ij] for part in parts]) for ij in UPPER}
        inside = m[0, 0] + m[1, 1] + m[2, 2]
        across = mu * inside
        for c, (i, j) in enumerate(UPPER):
            value = both * m[i, j] + across if i == j else both * m[i, j]
            start = pl.multiple_of(DIAG_BASE + c * DIAG_UP + group * 8, 8)
            k_ref[pl.ds(start, 8), :] = value
        return trace + jnp.where(row + group * 8 < NF, inside, 0.0)

    trace = lax.fori_loop(0, DIAG_UP // 8, diagonal, jnp.zeros((8, count), jnp.float32))
    local = jnp.sum((lam + 4.0 * mu) * trace)

    tail = lax.broadcasted_iota(jnp.int32, (WORDS - SLOT_WORD, count), 0)
    slots = slot_ref[...].astype(jnp.float32) + 1.0
    k_ref[SLOT_WORD:, :] = jnp.where(tail == 0, slots, 0.0)

    owners = lax.broadcasted_iota(jnp.int32, (ndevices, count), 0)
    mine = owner_ref[...] == owners
    onehot = mine.astype(jnp.bfloat16)
    before = (
        lax.broadcasted_iota(jnp.int32, (count, count), 0)
        < lax.broadcasted_iota(jnp.int32, (count, count), 1)
    ).astype(jnp.bfloat16)
    rank = jnp.dot(onehot, before, preferred_element_type=jnp.float32)
    place = jnp.sum(
        jnp.where(mine, owners * capacity + rank.astype(jnp.int32), 0), axis=0, keepdims=True
    )
    send = (lax.broadcasted_iota(jnp.int32, (width, count), 0) == place).astype(jnp.bfloat16)
    lane = lax.broadcasted_iota(jnp.int32, (width, LANES), 1)
    for tile in range(WORDS // LANES):
        words = slice(tile * LANES, (tile + 1) * LANES)
        moved = pick(send, k_ref[words, :], ((1,), (1,)))
        if tile == TRACE_WORD // LANES:
            moved = jnp.where(lane == TRACE_WORD % LANES, local, moved)
        out_ref[:, words] = moved


def owner_kernel(capacity, elements, in_ref, out_ref, sum_ref):
    width = in_ref.shape[0]
    tail = in_ref[:, WORDS - LANES :].T
    slots = tail[SLOT_WORD % LANES : SLOT_WORD % LANES + 1, :]
    traces = tail[TRACE_WORD % LANES : TRACE_WORD % LANES + 1, :]
    total = jnp.sum(traces) / capacity
    inverse = 1.0 / jnp.broadcast_to(total / (NDOF * elements), (SLOTS_DEV, LANES))
    wanted = (lax.broadcasted_iota(jnp.int32, (SLOTS_DEV, width), 0) + 1).astype(jnp.float32)
    placing = (slots == wanted).astype(jnp.bfloat16)
    for tile in range(WORDS // LANES):
        words = slice(tile * LANES, (tile + 1) * LANES)
        summed = pick(placing, in_ref[:, words], ((1,), (0,)))
        sum_ref[words, :] = (summed * inverse).T

    for a in range(NF):
        forth = NF // 2 if a < NF // 2 else NF // 2 - 1
        back = NF - 1 - forth
        runs = []
        near = min(forth, NF - 1 - a)
        runs.append((a + 1, a, NF, near, False))
        runs.append((0, (near) * NF + a, NF, forth - near, False))
        low = min(back, a)
        runs.append((a - low, None, low, low, True))
        runs.append((NF - (back - low), None, back, back - low, True))
        for i in range(3):
            m = 3 * a + i
            for j in range(3):
                for run in runs[:2]:
                    b, word, step, length, _ = run
                    if length:
                        out_ref[m, pl.ds(3 * b + j, length, stride=3), :] = sum_ref[
                            pl.ds((3 * i + j) * PAIRS_UP + word, length, stride=step), :
                        ]
                for b0, _, dmax, length, _ in runs[2:]:
                    for s in range(length):
                        d = dmax - s
                        b = (a - d) % NF
                        word = (3 * j + i) * PAIRS_UP + (d - 1) * NF + b
                        out_ref[m, 3 * b + j, :] = sum_ref[word, :]
                c = UPPER.index((min(i, j), max(i, j)))
                out_ref[m, 3 * a + j, :] = sum_ref[DIAG_BASE + c * DIAG_UP + a, :]


def shards(grads, weights, counts, lame_first, shear, dest_owner, dest_slot):
    points, _, _, count = grads.shape
    ndevices = lax.axis_size("row") * lax.axis_size("col")
    capacity = max(2, 2 * count // ndevices)
    width = ndevices * capacity
    g = jnp.transpose(grads, (1, 2, 0, 3)).reshape(NDOF, points, count)
    line = lambda v: v.reshape(1, count)
    payload = pl.pallas_call(
        functools.partial(element_kernel, ndevices, capacity),
        out_shape=jax.ShapeDtypeStruct((width, WORDS), jnp.float32),
        scratch_shapes=[
            pltpu.VMEM((NDOF, points, count), jnp.float32),
            pltpu.VMEM((WORDS, count), jnp.float32),
        ],
        name="elements",
    )(
        g,
        weights,
        line(counts),
        line(lame_first),
        line(shear),
        line(dest_owner),
        line(dest_slot),
    )
    moved = lax.all_to_all(
        payload.reshape(ndevices, capacity, WORDS), AXES, split_axis=0, concat_axis=0, tiled=True
    )
    return pl.pallas_call(
        functools.partial(owner_kernel, capacity, count * ndevices),
        out_shape=jax.ShapeDtypeStruct((NDOF, NDOF, SLOTS_DEV), jnp.float32),
        scratch_shapes=[pltpu.VMEM((WORDS, SLOTS_DEV), jnp.float32)],
        name="owners",
    )(moved.reshape(width, WORDS))


def solution(mesh):
    in_specs = (
        P(None, None, None, AXES),
        P(None, AXES),
        P(AXES),
        P(AXES),
        P(AXES),
        P(AXES, None),
        P(AXES),
    )
    out_specs = P(None, None, AXES)
    return jax.shard_map(shards, mesh=mesh, in_specs=in_specs, out_specs=out_specs, check_vma=False)
```

time: 144 us -> 67.7 us (0.47)
  local copies, waits for them, and re-layouts: 40.2 us -> 0 us
  matrix products: 16.2 us -> 0 us
  Pallas kernels: 0 us -> 14.1 us
  starting transfers between devices: 13.2 us -> 0 us
  blocking collectives: 65.9 us -> 53.3 us
  other arithmetic: 7.07 us -> 0 us
    psum x1 -> x0, blocking collectives: 65.9 us -> none  [shards(): total = lax.psum(local_trace, ('row', 'col'))]
    all_to_all x0 -> x1, blocking collectives: none -> 53.3 us  [shards(): lax.all_to_all(payload.reshape(ndevices, capacity, WORDS), AXES, split_ax...]
    dot_general x2 -> x0, matrix products: 16.2 us -> none  [the longest x1 12.3 us: stiffness(): jnp.einsum('qme,qne->mne', gflat * weff[:, None, :], gflat, precision=lax...]
    pallas_call x0 -> x2, Pallas kernels: none -> 14.1 us  [the longest x1 9.97 us: shards(): pl.pallas_call(functools.partial(element_kernel, ndevices, capacity), out...]
    gather x3 -> x0, local copies, waits for them, and re-layouts: 13.7 us -> none  [the longest x1 9.98 us: shards(): received = jnp.take(moved, jnp.asarray(mirror_index, jnp.int32), axis=0)]
    all_to_all x2 -> x0, starting transfers between devices: 13.2 us -> none  [the longest x1 7.33 us: deliver(): lax.all_to_all(slotcol, ('row', 'col'), split_axis=1, concat_axis=1, tile...]
    reshape x4 -> x0, local copies, waits for them, and re-layouts: 11.9 us -> none  [the longest x1 4.68 us: shards(): gflat = grads.reshape(Q, NDOF, count)]
    transpose x1 -> x0, local copies, waits for them, and re-layouts: 4.73 us -> none  [stiffness(): jnp.einsum('qme,qne->mne', gflat * weff[:, None, :], gflat, precision=lax...]
  transfers between devices with their start and end apart: 2 -> 0, of which waited for: 0 -> 0; matrix products, arithmetic and copies ran while one was open for 28% -> 0% of each run, Pallas kernels for 0% -> 0%
where the time goes in v1:
time: 67.7 us; the launch traced here: 67.4 us
  blocking collectives  53.3 us (79%)
  Pallas kernels  14.1 us (21%)
    all_to_all x1, blocking collectives, shards(): lax.all_to_all(payload.reshape(ndevices, capacity, WORDS), AXES, split_ax...  53.3 us
    pallas_call x1, Pallas kernels, shards(): pl.pallas_call(functools.partial(element_kernel, ndevices, capacity), out...  9.97 us
    pallas_call x1, Pallas kernels, shards(): pl.pallas_call(functools.partial(owner_kernel, capacity, count * ndevices...  4.15 us

profile of v1, /device:TPU:0, one launch (start us, length us, event | category | flops | bytes accessed | tf_op | source)
XLA Modules:
  0.0 67.4 jit_solution(12288532294395780489)
XLA Ops:
  0.0 10.0 %elements.1 = f32[256,1920]{1,0:T(8,128)} custom-call(f32[60,64,128]{2,1,0:T(8,128)} %bitcast.12, f32[64,128]{1,0:T(8,128)} %w_ref.1, s32[1,128]{1,0:T(1,128)} %bitcast.13, f32[1,128]{1,0:T(1,128)} %bitcast.14, f32[1,128]{1,0:T(1,128)} %bitcast.15, s32[1,128]{1,0:T(1,128)} %bitcast.16, s32[1,128]{1,0:T(1,128)} %bitcast.17), custom_call_target="tpu_custom_call" | custom-call | tf_op jit(solution)/shard_map/elements/pallas_call | solution.py:207
  10.0 53.3 %all_to_all.5 = f32[32,8,1920]{2,1,0:T(8,128)} all-to-all(f32[32,8,1920]{2,1,0:T(8,128)} %bitcast.11), channel_id=1, replica_groups=mesh['row'=8,'col'=4] {'row','col'}, dimensions={0} | all-to-all | bytes 3932160 | tf_op jit(solution)/shard_map/all_to_all | solution.py:224
  63.3 4.2 %owners.1 = f32[60,60,128]{2,1,0:T(8,128)} custom-call(f32[256,1920]{1,0:T(8,128)} %bitcast.10), custom_call_target="tpu_custom_call" | custom-call | tf_op jit(solution)/shard_map/owners/pallas_call | solution.py:227

commit v2 on v1

v2 whole, which is shorter than its diff:
```python
import functools

import jax
import jax.numpy as jnp
from jax import lax
from jax.experimental import pallas as pl
from jax.experimental.pallas import tpu as pltpu
from jax.sharding import PartitionSpec as P


NF = 20
NDOF = 60
GP = 8
SLOTS_DEV = 128
LANES = 128
STRIPES = 4
AXES = ("row", "col")

FULL = tuple((i, j) for i in range(3) for j in range(3))
UPPER = ((0, 0), (0, 1), (0, 2), (1, 1), (1, 2), (2, 2))
DIAG_UP = -(-NF // 8) * 8


class Part:
    def __init__(self, first, last, inner, leads):
        self.first, self.last, self.inner, self.leads = first, last, inner, leads
        pairs = sum(NF // 2 if 2 * d == NF else NF for d in range(first, last + 1))
        self.pairs = -(-pairs // 8) * 8
        self.diagonal = 9 * self.pairs
        self.used = self.diagonal + len(inner) * DIAG_UP
        self.slot = self.diagonal + NF if inner else self.used
        self.trace = self.slot + 1
        self.words = -(-(self.used + 2 * leads) // LANES) * LANES


LEAD = Part(1, 4, (), True)
REST = Part(5, 10, UPPER, False)


def split(value):
    high = value.astype(jnp.bfloat16)
    low = (value - high.astype(jnp.float32)).astype(jnp.bfloat16)
    return high, low


def pick(onehot, value, dims):
    high, low = split(value)
    dot = functools.partial(
        lax.dot_general, dimension_numbers=(dims, ((), ())), preferred_element_type=jnp.float32
    )
    return dot(onehot, high) + dot(onehot, low)


def fold(parts):
    row = lax.broadcasted_iota(jnp.int32, parts[0].shape, 0)
    for bit in (1, 2, 4):
        keep = (row & bit) == 0
        parts = [
            jnp.where(keep, first, second)
            + pltpu.roll(jnp.where(keep, second, first), 8 - bit, 0)
            for first, second in zip(parts[0::2], parts[1::2])
        ]
    return parts[0]


def lead_elements(plane, ndevices, capacity, *refs):
    g_hbm, w_hbm, counts_hbm, lame_hbm, shear_hbm, slot_hbm, owner_hbm = refs[:7]
    *out_refs, place_ref, g_ref, wg_ref, lines_ref = refs[7:-8]
    w_ref, counts_ref, lame_ref, shear_ref, slot_ref, owner_ref, k_ref, sems = refs[-8:]
    points, count = w_ref.shape
    width = ndevices * capacity
    small = [
        pltpu.make_async_copy(source, target, sems.at[n])
        for n, (source, target) in enumerate(
            (
                (w_hbm, w_ref),
                (counts_hbm, counts_ref),
                (lame_hbm, lame_ref),
                (shear_hbm, shear_ref),
                (slot_hbm, slot_ref),
                (owner_hbm, owner_ref),
            )
        )
    ]
    stripe = NDOF // STRIPES
    large = [
        pltpu.make_async_copy(
            g_hbm.at[pl.ds(n * stripe, stripe)],
            g_ref.at[pl.ds(n * stripe, stripe)],
            sems.at[len(small) + n],
        )
        for n in range(STRIPES)
    ]
    for copy in small + large:
        copy.start()
    for copy in small:
        copy.wait()

    owners = lax.broadcasted_iota(jnp.int32, (ndevices, count), 0)
    mine = owner_ref[...] == owners
    before = (
        lax.broadcasted_iota(jnp.int32, (count, count), 0)
        < lax.broadcasted_iota(jnp.int32, (count, count), 1)
    ).astype(jnp.bfloat16)
    rank = jnp.dot(
        mine.astype(jnp.bfloat16), before, preferred_element_type=jnp.float32
    ).astype(jnp.int32)

    def place(base):
        return jnp.sum(jnp.where(mine, base * capacity + rank, 0), axis=0, keepdims=True)

    place_ref[...] = place(owners)
    me = lax.axis_index("row") * lax.axis_size("col") + lax.axis_index("col")
    ahead = owners // plane - me // plane
    ahead = jnp.where(ahead < 0, ahead + ndevices // plane, ahead)
    aside = owners % plane - me % plane
    aside = jnp.where(aside < 0, aside + plane, aside)
    where = place(ahead * plane + aside)

    qrow = lax.broadcasted_iota(jnp.int32, (points, count), 0)
    weff = jnp.where(qrow < counts_ref[...] * GP, w_ref[...], 0.0)

    def weigh(m, inside):
        g = g_ref[m]
        weighted = g * weff
        wg_ref[m] = weighted
        return inside + jnp.sum((weighted * g).reshape(points // 8, 8, count), axis=0)

    inside = jnp.zeros((8, count), jnp.float32)
    for n, copy in enumerate(large):
        copy.wait()
        inside = lax.fori_loop(n * stripe, (n + 1) * stripe, weigh, inside, unroll=3)
    slots = slot_ref[...].astype(jnp.float32) + 1.0
    row = lax.broadcasted_iota(jnp.int32, (8, count), 0)
    lam = jnp.broadcast_to(lame_ref[...], (8, count))
    mu = jnp.broadcast_to(shear_ref[...], (8, count))
    lines_ref[...] = jnp.where(row == 0, lam, jnp.where(row == 1, mu, slots))
    local = jnp.sum((lam + 4.0 * mu) * inside)
    blocks(LEAD, g_ref, wg_ref, lam, mu, slots[:1], k_ref)

    lane = lax.broadcasted_iota(jnp.int32, (width, LANES), 1)
    rows = plane * capacity
    for words, moved in selected(LEAD, where, width, k_ref):
        if words.start == LEAD.trace // LANES * LANES:
            moved = jnp.where(lane == LEAD.trace % LANES, local, moved)
        for k, out_ref in enumerate(out_refs):
            out_ref[:, words] = moved[k * rows : (k + 1) * rows]


def rest_elements(g_ref, wg_ref, lines_ref, place_ref, out_ref, k_ref):
    lam, mu, slots = (jnp.broadcast_to(lines_ref[n : n + 1, :], (8, k_ref.shape[1])) for n in range(3))
    blocks(REST, g_ref, wg_ref, lam, mu, slots[:1], k_ref)
    for words, moved in selected(REST, place_ref[...], out_ref.shape[0], k_ref):
        out_ref[:, words] = moved


def selected(part, where, width, k_ref):
    send = (lax.broadcasted_iota(jnp.int32, (width, k_ref.shape[1]), 0) == where).astype(
        jnp.bfloat16
    )
    for tile in range(part.words // LANES):
        words = slice(tile * LANES, (tile + 1) * LANES)
        yield words, pick(send, k_ref[words, :], ((1,), (1,)))


def blocks(part, g_ref, wg_ref, lam, mu, slots, k_ref):
    points, count = g_ref.shape[1:]
    both = lam + mu

    def products(a, b, wanted):
        sums = {}
        for t in range(points // 8):
            rows = pl.ds(8 * t, 8)
            left = [wg_ref[3 * a + i, rows, :] for i in range(3)]
            right = [g_ref[3 * b + j, rows, :] for j in range(3)]
            for i, j in wanted:
                term = left[i] * right[j]
                sums[i, j] = term if t == 0 else sums[i, j] + term
        return sums

    def off_diagonal(group, carry):
        sums = []
        for k in range(8):
            p = group * 8 + k
            d = p // NF
            a = p - d * NF
            b = a + d + part.first
            b = jnp.where(b >= NF, b - NF, b)
            sums.append(products(a, b, FULL))
        m = {ij: fold([one[ij] for one in sums]) for ij in FULL}
        across = mu * (m[0, 0] + m[1, 1] + m[2, 2])
        for i, j in FULL:
            value = both * m[i, i] + across if i == j else lam * m[i, j] + mu * m[j, i]
            start = pl.multiple_of((3 * i + j) * part.pairs + group * 8, 8)
            k_ref[pl.ds(start, 8), :] = value
        return carry

    lax.fori_loop(0, part.pairs // 8, off_diagonal, 0)

    def diagonal(group, carry):
        sums = []
        for k in range(8):
            a = jnp.minimum(group * 8 + k, NF - 1)
            sums.append(products(a, a, part.inner))
        m = {ij: fold([one[ij] for one in sums]) for ij in part.inner}
        if (0, 0) in part.inner:
            across = mu * (m[0, 0] + m[1, 1] + m[2, 2])
        for c, (i, j) in enumerate(part.inner):
            value = both * m[i, j] + across if i == j else both * m[i, j]
            start = pl.multiple_of(part.diagonal + c * DIAG_UP + group * 8, 8)
            k_ref[pl.ds(start, 8), :] = value
        return carry

    if part.inner:
        lax.fori_loop(0, DIAG_UP // 8, diagonal, 0)

    if part.used < part.words:
        k_ref[pl.ds(part.used, part.words - part.used), :] = jnp.zeros(
            (part.words - part.used, count), jnp.float32
        )
    k_ref[pl.ds(part.slot, 1), :] = slots


def gather_words(part, inverse, in_ref, sum_ref):
    width = in_ref.shape[0]
    base = part.slot // LANES * LANES
    tail = in_ref[:, base : base + LANES].T
    slots = tail[part.slot - base : part.slot - base + 1, :]
    wanted = (lax.broadcasted_iota(jnp.int32, (SLOTS_DEV, width), 0) + 1).astype(jnp.float32)
    placing = (slots == wanted).astype(jnp.bfloat16)
    for tile in range(part.words // LANES):
        words = slice(tile * LANES, (tile + 1) * LANES)
        summed = pick(placing, in_ref[:, words], ((1,), (0,)))
        sum_ref[words, :] = (summed * inverse).T


def relay_kernel(plane, capacity, *refs):
    planes = len(refs) - plane
    in_refs, out_refs = refs[:planes], refs[planes:]
    for l, out_ref in enumerate(out_refs):
        for k, in_ref in enumerate(in_refs):
            out_ref[k * capacity : (k + 1) * capacity] = in_ref[l * capacity : (l + 1) * capacity]


def lead_kernel(part, capacity, elements, *refs):
    in_refs, (sum_ref, inverse_ref, all_ref) = refs[:-3], refs[-3:]
    rows = in_refs[0].shape[0]
    for l, in_ref in enumerate(in_refs):
        all_ref[l * rows : (l + 1) * rows] = in_ref[...]
    total = jnp.sum(all_ref[:, part.trace : part.trace + 1]) / capacity
    inverse = 1.0 / jnp.broadcast_to(total / (NDOF * elements), (SLOTS_DEV, LANES))
    inverse_ref[...] = inverse
    gather_words(part, inverse, all_ref, sum_ref)


def last_kernel(in_ref, inverse_ref, lead_ref, out_ref, sum_ref, whole_ref, sems):
    gather_words(REST, inverse_ref[...], in_ref, sum_ref)
    sums = {LEAD: lead_ref, REST: sum_ref}

    def copy(stripe):
        rows = pl.ds(stripe * (NDOF // STRIPES), NDOF // STRIPES)
        return pltpu.make_async_copy(whole_ref.at[rows], out_ref.at[rows], sems.at[stripe])

    for a in range(NF):
        forth = NF // 2 if a < NF // 2 else NF // 2 - 1
        back = NF - 1 - forth
        for i in range(3):
            m = 3 * a + i
            for j in range(3):
                for one, ref in sums.items():
                    for d in range(one.first, one.last + 1):
                        start = (d - one.first) * NF
                        if d <= forth:
                            b = (a + d) % NF
                            word = (3 * i + j) * one.pairs + start + a
                            whole_ref[m, 3 * b + j, :] = ref[word, :]
                        if d <= back:
                            b = (a - d) % NF
                            word = (3 * j + i) * one.pairs + start + b
                            whole_ref[m, 3 * b + j, :] = ref[word, :]
                    ij = (min(i, j), max(i, j))
                    if ij in one.inner:
                        word = one.diagonal + one.inner.index(ij) * DIAG_UP + a
                        whole_ref[m, 3 * a + j, :] = ref[word, :]
        if (a + 1) * STRIPES % NF == 0:
            copy((a + 1) * STRIPES // NF - 1).start()
    for stripe in range(STRIPES):
        copy(stripe).wait()


def shards(grads, weights, counts, lame_first, shear, dest_owner, dest_slot):
    points, _, _, count = grads.shape
    nrow, ncol = lax.axis_size("row"), lax.axis_size("col")
    ndevices = nrow * ncol
    capacity = max(2, 2 * count // ndevices)
    width = ndevices * capacity
    planes = nrow // 2 if nrow % 2 == 0 else nrow
    plane = ndevices // planes
    f32 = lambda *shape: jax.ShapeDtypeStruct(shape, jnp.float32)
    line = lambda v: v.reshape(1, count)
    params = pltpu.CompilerParams(vmem_limit_bytes=20 * 2**20)
    vmem = pltpu.VMEM
    hbm = pl.BlockSpec(memory_space=pltpu.MemorySpace.HBM)
    large = (NDOF, points, count)

    near = lambda d, k: (d + k * plane) % ndevices
    beside = lambda d, l: d // plane * plane + (d + l) % plane
    cost = lambda part: pl.CostEstimate(
        flops=60000 * part.words, bytes_accessed=4000000, transcendentals=0
    )
    *blocks, place, g, wg, lines = pl.pallas_call(
        functools.partial(lead_elements, plane, ndevices, capacity),
        in_specs=[hbm] * 7,
        out_shape=[f32(plane * capacity, LEAD.words)] * planes
        + [jax.ShapeDtypeStruct((1, count), jnp.int32), f32(*large), f32(*large), f32(8, count)],
        scratch_shapes=[
            vmem((points, count), jnp.float32),
            vmem((1, count), jnp.int32),
            vmem((1, count), jnp.float32),
            vmem((1, count), jnp.float32),
            vmem((1, count), jnp.int32),
            vmem((1, count), jnp.int32),
            vmem((LEAD.words, count), jnp.float32),
            pltpu.SemaphoreType.DMA((6 + STRIPES,)),
        ],
        compiler_params=params,
        cost_estimate=cost(LEAD),
        name="elements_lead",
    )(
        *(
            pltpu.with_memory_space_constraint(v, pltpu.MemorySpace.HBM)
            for v in (
                jnp.transpose(grads, (1, 2, 0, 3)).reshape(large),
                weights,
                line(counts),
                line(lame_first),
                line(shear),
                line(dest_slot),
                line(dest_owner),
            )
        )
    )
    for k in range(1, planes):
        pairs = [(d, near(d, k)) for d in range(ndevices)]
        blocks[k] = lax.ppermute(blocks[k], AXES, pairs)
    rest = pl.pallas_call(
        rest_elements,
        out_shape=f32(width, REST.words),
        scratch_shapes=[vmem((REST.words, count), jnp.float32)],
        compiler_params=params,
        cost_estimate=cost(REST),
        name="elements_rest",
    )(g, wg, lines, place)
    rest = lax.all_to_all(
        rest.reshape(ndevices, capacity, REST.words),
        AXES,
        split_axis=0,
        concat_axis=0,
        tiled=True,
    ).reshape(width, REST.words)
    blocks = pl.pallas_call(
        functools.partial(relay_kernel, plane, capacity),
        out_shape=[f32(planes * capacity, LEAD.words)] * plane,
        compiler_params=params,
        name="relay",
    )(*blocks)
    blocks = list(blocks)
    for l in range(1, plane):
        pairs = [(d, beside(d, l)) for d in range(ndevices)]
        blocks[l] = lax.ppermute(blocks[l], AXES, pairs)
    lead, inverse = pl.pallas_call(
        functools.partial(lead_kernel, LEAD, capacity, count * ndevices),
        out_shape=[f32(LEAD.words, SLOTS_DEV), f32(SLOTS_DEV, LANES)],
        scratch_shapes=[pltpu.VMEM((width, LEAD.words), jnp.float32)],
        compiler_params=params,
        name="owners_lead",
    )(*blocks)
    return pl.pallas_call(
        last_kernel,
        out_shape=f32(NDOF, NDOF, SLOTS_DEV),
        out_specs=pl.BlockSpec(memory_space=pl.ANY),
        scratch_shapes=[
            pltpu.VMEM((REST.words, SLOTS_DEV), jnp.float32),
            pltpu.VMEM((NDOF, NDOF, SLOTS_DEV), jnp.float32),
            pltpu.SemaphoreType.DMA((STRIPES,)),
        ],
        compiler_params=params,
        name="owners_last",
    )(rest, inverse, lead)


def solution(mesh):
    in_specs = (
        P(None, None, None, AXES),
        P(None, AXES),
        P(AXES),
        P(AXES),
        P(AXES),
        P(AXES, None),
        P(AXES),
    )
    out_specs = P(None, None, AXES)

    return jax.shard_map(shards, mesh=mesh, in_specs=in_specs, out_specs=out_specs, check_vma=False)
```

time: 67.7 us -> 79.2 us (1.17)
  the two profiles are of different devices: /device:TPU:0 before, /device:TPU:11 now
where the time goes in v2:
time: 79.2 us; the launch traced here: 79 us
  waiting for transfers between devices  46.7 us (59%)
  starting transfers between devices  16.9 us (21%)
  Pallas kernels  15.3 us (19%)
    ppermute x3, waiting for transfers between devices, shards(): blocks[k] = lax.ppermute(blocks[k], AXES, pairs)  40.5 us
    ppermute x7, starting transfers between devices, shards(): blocks[l] = lax.ppermute(blocks[l], AXES, pairs)  6.96 us
    pallas_call x1, Pallas kernels, shards(): pl.pallas_call(rest_elements, out_shape=f32(width, REST.words), scratch_s...  6.59 us
    all_to_all x1, starting transfers between devices, shards(): lax.all_to_all(rest.reshape(ndevices, capacity, REST.words), AXES, split_...  6.3 us
    ppermute x7, waiting for transfers between devices, shards(): blocks[l] = lax.ppermute(blocks[l], AXES, pairs)  6.28 us
    pallas_call x1, Pallas kernels, shards(): pl.pallas_call(functools.partial(lead_elements, plane, ndevices, capacity...  5.59 us
    ppermute x3, starting transfers between devices, shards(): blocks[k] = lax.ppermute(blocks[k], AXES, pairs)  3.67 us
    pallas_call x1, Pallas kernels, shards(): pl.pallas_call(last_kernel, out_shape=f32(NDOF, NDOF, SLOTS_DEV), out_spe...  2.54 us
  transfers between devices with their start and end apart: 11, of which 5 were waited for; matrix products, arithmetic and copies ran while one was open for 0% of the time, Pallas kernels for 1%

profile of v2, /device:TPU:11, one launch (start us, length us, event | category | flops | bytes accessed | tf_op | source)
XLA Modules:
  0.0 79.0 jit_solution(17459852429117950879)
XLA Ops:
  0.0 5.6 %elements_lead.1 = (f32[64,768]{1,0:T(8,128)S(1)}, f32[64,768]{1,0:T(8,128)S(1)}, f32[64,768]{1,0:T(8,128)S(1)}, f32[64,768]{1,0:T(8,128)S(1)}, s32[1,128]{1,0:T...) custom-call(f32[60,64,128]{2,1,0:T(8,128)} %bitcast.11, ...), custom_call_target="tpu_custom_call" | custom-call | flops 46080000 | bytes 4000000 | tf_op jit(solution)/shard_map/elements_lead/pallas_call | solution.py:311
  5.6 6.6 %elements_rest.1 = f32[256,1152]{1,0:T(8,128)} custom-call(f32[60,64,128]{2,1,0:T(8,128)S(1)} %get-tuple-element.23.g_ref, f32[60,64,128]{2,1,0:T(8,128)S(1)} %get-tuple-element.24.wg_ref, f32[8,128]{1,0:T(8,128)S(1)} %get-tuple-element.25.lines_ref, s32[1,128]{1,0:T(1,128)S(1)} %get-tuple-element.26.place_ref), custom_call_target="tpu_custom_call" | custom-call | flops 69120000 | bytes 4000000 | tf_op jit(solution)/shard_map/elements_rest/pallas_call | solution.py:346
  12.2 6.3 %all-to-all-start = ((f32[32,8,1152]{2,1,0:T(8,128)}), f32[32,8,1152]{2,1,0:T(8,128)S(1)}, u32[]{:S(2)}, u32[]{:S(2)}) async-start(f32[32,8,1152]{2,1,0:T(8,128)} %bitcast.7), calls=%async_computation | async-start | bytes 2359296 | tf_op jit(solution)/shard_map/all_to_all | solution.py:354
  18.5 1.2 %collective-permute-start = (f32[64,768]{1,0:T(8,128)S(1)}, f32[64,768]{1,0:T(8,128)S(1)}, u32[]{:S(2)}, u32[]{:S(2)}) collective-permute-start(f32[64,768]{1,0:T(8,128)S(1)} %get-tuple-element.28), channel_id=1, source_target_pairs={{0,8},{1,9},{2,10},{3,11},{4,12},{5,13},{6,14},{7,15},{8,16},{9,17... | collective-permute-start | bytes 589832 | tf_op jit(solution)/shard_map/ppermute | solution.py:345
  19.7 1.2 %collective-permute-start.1 = (f32[64,768]{1,0:T(8,128)S(1)}, f32[64,768]{1,0:T(8,128)S(1)}, u32[]{:S(2)}, u32[]{:S(2)}) collective-permute-start(f32[64,768]{1,0:T(8,128)S(1)} %get-tuple-element.29), channel_id=1, source_target_pairs={{0,16},{1,17},{2,18},{3,19},{4,20},{5,21},{6,22},{7,23},{8,24},{9,... | collective-permute-start | bytes 589832 | tf_op jit(solution)/shard_map/ppermute | solution.py:345
  20.9 1.3 %collective-permute-start.2 = (f32[64,768]{1,0:T(8,128)S(1)}, f32[64,768]{1,0:T(8,128)S(1)}, u32[]{:S(2)}, u32[]{:S(2)}) collective-permute-start(f32[64,768]{1,0:T(8,128)S(1)} %get-tuple-element.30), channel_id=1, source_target_pairs={{0,24},{1,25},{2,26},{3,27},{4,28},{5,29},{6,30},{7,31},{8,0},{9,1... | collective-permute-start | bytes 589832 | tf_op jit(solution)/shard_map/ppermute | solution.py:345
  22.2 34.4 %collective-permute-done.refs_1_ = f32[64,768]{1,0:T(8,128)S(1)} collective-permute-done((f32[64,768]{1,0:T(8,128)S(1)}, f32[64,768]{1,0:T(8,128)S(1)}, u32[]{:S(2)}, u32[]{:S(2)}) %collective-permute-start) | collective-permute-done | bytes 196640 | tf_op jit(solution)/shard_map/ppermute | solution.py:345
  56.5 4.2 %collective-permute-done.1.refs_2_ = f32[64,768]{1,0:T(8,128)S(1)} collective-permute-done((f32[64,768]{1,0:T(8,128)S(1)}, f32[64,768]{1,0:T(8,128)S(1)}, u32[]{:S(2)}, u32[]{:S(2)}) %collective-permute-start.1) | collective-permute-done | bytes 196640 | tf_op jit(solution)/shard_map/ppermute | solution.py:345
  60.7 1.9 %collective-permute-done.2.refs_3_ = f32[64,768]{1,0:T(8,128)S(1)} collective-permute-done((f32[64,768]{1,0:T(8,128)S(1)}, f32[64,768]{1,0:T(8,128)S(1)}, u32[]{:S(2)}, u32[]{:S(2)}) %collective-permute-start.2) | collective-permute-done | bytes 196640 | tf_op jit(solution)/shard_map/ppermute | solution.py:345
  62.6 0.1 relay.1
  62.7 2.1 %collective-permute-start.3 = (f32[32,768]{1,0:T(8,128)S(1)}, f32[32,768]{1,0:T(8,128)S(1)}, u32[]{:S(2)}, u32[]{:S(2)}) collective-permute-start(f32[32,768]{1,0:T(8,128)S(1)} %get-tuple-element.32), channel_id=1, source_target_pairs={{0,1},{1,2},{2,3},{3,4},{4,5},{5,6},{6,7},{7,0},{8,9},{9,10},{10,1... | collective-permute-start | bytes 294920 | tf_op jit(solution)/shard_map/ppermute | solution.py:370
  64.7 1.2 %collective-permute-start.4 = (f32[32,768]{1,0:T(8,128)S(1)}, f32[32,768]{1,0:T(8,128)S(1)}, u32[]{:S(2)}, u32[]{:S(2)}) collective-permute-start(f32[32,768]{1,0:T(8,128)S(1)} %get-tuple-element.33), channel_id=1, source_target_pairs={{0,2},{1,3},{2,4},{3,5},{4,6},{5,7},{6,0},{7,1},{8,10},{9,11},{10,... | collective-permute-start | bytes 294920 | tf_op jit(solution)/shard_map/ppermute | solution.py:370
  65.9 0.0 collective-permute-start.5
  65.9 0.6 collective-permute-start.6
  66.6 1.7 %collective-permute-start.7 = (f32[32,768]{1,0:T(8,128)S(1)}, f32[32,768]{1,0:T(8,128)S(1)}, u32[]{:S(2)}, u32[]{:S(2)}) collective-permute-start(f32[32,768]{1,0:T(8,128)S(1)} %get-tuple-element.36), channel_id=1, source_target_pairs={{0,5},{1,6},{2,7},{3,0},{4,1},{5,2},{6,3},{7,4},{8,13},{9,14},{10,... | collective-permute-start | bytes 294920 | tf_op jit(solution)/shard_map/ppermute | solution.py:370
  68.3 0.0 collective-permute-done.3.refs_1_
  68.3 1.1 %collective-permute-start.8 = (f32[32,768]{1,0:T(8,128)S(1)}, f32[32,768]{1,0:T(8,128)S(1)}, u32[]{:S(2)}, u32[]{:S(2)}) collective-permute-start(f32[32,768]{1,0:T(8,128)S(1)} %get-tuple-element.37), channel_id=1, source_target_pairs={{0,6},{1,7},{2,0},{3,1},{4,2},{5,3},{6,4},{7,5},{8,14},{9,15},{10,... | collective-permute-start | bytes 294920 | tf_op jit(solution)/shard_map/ppermute | solution.py:370
  69.4 0.0 collective-permute-done.4.refs_2_
  69.4 0.3 collective-permute-start.9
  69.7 0.9 %collective-permute-done.5.refs_3_ = f32[32,768]{1,0:T(8,128)S(1)} collective-permute-done((f32[32,768]{1,0:T(8,128)S(1)}, f32[32,768]{1,0:T(8,128)S(1)}, u32[]{:S(2)}, u32[]{:S(2)}) %collective-permute-start.5) | collective-permute-done | bytes 98336 | tf_op jit(solution)/shard_map/ppermute | solution.py:370
  70.5 0.0 collective-permute-done.6.refs_4_
  70.5 5.4 %collective-permute-done.7.refs_5_ = f32[32,768]{1,0:T(8,128)S(1)} collective-permute-done((f32[32,768]{1,0:T(8,128)S(1)}, f32[32,768]{1,0:T(8,128)S(1)}, u32[]{:S(2)}, u32[]{:S(2)}) %collective-permute-start.7) | collective-permute-done | bytes 98336 | tf_op jit(solution)/shard_map/ppermute | solution.py:370
  75.9 0.0 collective-permute-done.8.refs_6_
  75.9 0.0 collective-permute-done.9.refs_7_
  75.9 0.5 owners_lead.1
  76.5 0.0 all-to-all-done
  76.5 2.5 %owners_last.1 = f32[60,60,128]{2,1,0:T(8,128)} custom-call(f32[256,1152]{1,0:T(8,128)S(1)} %bitcast.10, f32[128,128]{1,0:T(8,128)S(1)} %get-tuple-element.39.inverse_ref, f32[768,128]{1,0:T(8,128)S(1)} %get-tuple-element.40.lead_ref), custom_call_target="tpu_custom_call" | custom-call | tf_op jit(solution)/shard_map/owners_last/pallas_call | solution.py:378
Async XLA Ops:
  12.2 64.3 %all-to-all-start = ((f32[32,8,1152]{2,1,0:T(8,128)}), f32[32,8,1152]{2,1,0:T(8,128)S(1)}, u32[]{:S(2)}, u32[]{:S(2)}) async-start(f32[32,8,1152]{2,1,0:T(8,128)} %bitcast.7), calls=%async_computation | async-start | bytes 2359296 | tf_op jit(solution)/shard_map/all_to_all | solution.py:354
  18.5 38.0 %collective-permute-start = (f32[64,768]{1,0:T(8,128)S(1)}, f32[64,768]{1,0:T(8,128)S(1)}, u32[]{:S(2)}, u32[]{:S(2)}) collective-permute-start(f32[64,768]{1,0:T(8,128)S(1)} %get-tuple-element.28), channel_id=1, source_target_pairs={{0,8},{1,9},{2,10},{3,11},{4,12},{5,13},{6,14},{7,15},{8,16},{9,17... | collective-permute-start | bytes 589832 | tf_op jit(solution)/shard_map/ppermute | solution.py:345
  19.7 41.0 %collective-permute-start.1 = (f32[64,768]{1,0:T(8,128)S(1)}, f32[64,768]{1,0:T(8,128)S(1)}, u32[]{:S(2)}, u32[]{:S(2)}) collective-permute-start(f32[64,768]{1,0:T(8,128)S(1)} %get-tuple-element.29), channel_id=1, source_target_pairs={{0,16},{1,17},{2,18},{3,19},{4,20},{5,21},{6,22},{7,23},{8,24},{9,... | collective-permute-start | bytes 589832 | tf_op jit(solution)/shard_map/ppermute | solution.py:345
  20.9 41.7 %collective-permute-start.2 = (f32[64,768]{1,0:T(8,128)S(1)}, f32[64,768]{1,0:T(8,128)S(1)}, u32[]{:S(2)}, u32[]{:S(2)}) collective-permute-start(f32[64,768]{1,0:T(8,128)S(1)} %get-tuple-element.30), channel_id=1, source_target_pairs={{0,24},{1,25},{2,26},{3,27},{4,28},{5,29},{6,30},{7,31},{8,0},{9,1... | collective-permute-start | bytes 589832 | tf_op jit(solution)/shard_map/ppermute | solution.py:345
  62.7 5.6 %collective-permute-start.3 = (f32[32,768]{1,0:T(8,128)S(1)}, f32[32,768]{1,0:T(8,128)S(1)}, u32[]{:S(2)}, u32[]{:S(2)}) collective-permute-start(f32[32,768]{1,0:T(8,128)S(1)} %get-tuple-element.32), channel_id=1, source_target_pairs={{0,1},{1,2},{2,3},{3,4},{4,5},{5,6},{6,7},{7,0},{8,9},{9,10},{10,1... | collective-permute-start | bytes 294920 | tf_op jit(solution)/shard_map/ppermute | solution.py:370
  64.7 4.7 %collective-permute-start.4 = (f32[32,768]{1,0:T(8,128)S(1)}, f32[32,768]{1,0:T(8,128)S(1)}, u32[]{:S(2)}, u32[]{:S(2)}) collective-permute-start(f32[32,768]{1,0:T(8,128)S(1)} %get-tuple-element.33), channel_id=1, source_target_pairs={{0,2},{1,3},{2,4},{3,5},{4,6},{5,7},{6,0},{7,1},{8,10},{9,11},{10,... | collective-permute-start | bytes 294920 | tf_op jit(solution)/shard_map/ppermute | solution.py:370
  65.9 4.6 %collective-permute-start.5 = (f32[32,768]{1,0:T(8,128)S(1)}, f32[32,768]{1,0:T(8,128)S(1)}, u32[]{:S(2)}, u32[]{:S(2)}) collective-permute-start(f32[32,768]{1,0:T(8,128)S(1)} %get-tuple-element.34), channel_id=1, source_target_pairs={{0,3},{1,4},{2,5},{3,6},{4,7},{5,0},{6,1},{7,2},{8,11},{9,12},{10,... | collective-permute-start | bytes 294920 | tf_op jit(solution)/shard_map/ppermute | solution.py:370
  65.9 4.6 %collective-permute-start.6 = (f32[32,768]{1,0:T(8,128)S(1)}, f32[32,768]{1,0:T(8,128)S(1)}, u32[]{:S(2)}, u32[]{:S(2)}) collective-permute-start(f32[32,768]{1,0:T(8,128)S(1)} %get-tuple-element.35), channel_id=1, source_target_pairs={{0,4},{1,5},{2,6},{3,7},{4,0},{5,1},{6,2},{7,3},{8,12},{9,13},{10,... | collective-permute-start | bytes 294920 | tf_op jit(solution)/shard_map/ppermute | solution.py:370
  66.6 9.4 %collective-permute-start.7 = (f32[32,768]{1,0:T(8,128)S(1)}, f32[32,768]{1,0:T(8,128)S(1)}, u32[]{:S(2)}, u32[]{:S(2)}) collective-permute-start(f32[32,768]{1,0:T(8,128)S(1)} %get-tuple-element.36), channel_id=1, source_target_pairs={{0,5},{1,6},{2,7},{3,0},{4,1},{5,2},{6,3},{7,4},{8,13},{9,14},{10,... | collective-permute-start | bytes 294920 | tf_op jit(solution)/shard_map/ppermute | solution.py:370
  68.3 7.7 %collective-permute-start.8 = (f32[32,768]{1,0:T(8,128)S(1)}, f32[32,768]{1,0:T(8,128)S(1)}, u32[]{:S(2)}, u32[]{:S(2)}) collective-permute-start(f32[32,768]{1,0:T(8,128)S(1)} %get-tuple-element.37), channel_id=1, source_target_pairs={{0,6},{1,7},{2,0},{3,1},{4,2},{5,3},{6,4},{7,5},{8,14},{9,15},{10,... | collective-permute-start | bytes 294920 | tf_op jit(solution)/shard_map/ppermute | solution.py:370
  69.4 6.5 %collective-permute-start.9 = (f32[32,768]{1,0:T(8,128)S(1)}, f32[32,768]{1,0:T(8,128)S(1)}, u32[]{:S(2)}, u32[]{:S(2)}) collective-permute-start(f32[32,768]{1,0:T(8,128)S(1)} %get-tuple-element.38), channel_id=1, source_target_pairs={{0,7},{1,0},{2,1},{3,2},{4,3},{5,4},{6,5},{7,6},{8,15},{9,8},{10,9... | collective-permute-start | bytes 294920 | tf_op jit(solution)/shard_map/ppermute | solution.py:370

commit v3 on v2

--- a/solution.py
+++ b/solution.py
@@ -14,6 +14,7 @@
 SLOTS_DEV = 128
 LANES = 128
 STRIPES = 4
+HOPS = lambda planes: range(1, planes)
 AXES = ("row", "col")
 
 FULL = tuple((i, j) for i in range(3) for j in range(3))
@@ -21,20 +22,43 @@
 DIAG_UP = -(-NF // 8) * 8
 
 
+def near_pairs(offset):
+    def double(t):
+        a, d = t % NF, offset + t // NF * 2
+        return a, (a + d) % NF, (a + d + 1) % NF
+
+    return double
+
+
+def far_pairs(t):
+    v = lambda k: 9 * k % NF
+    m = t // 2 * 4 + 2 + t % 2
+    c = (t - NF // 2) * 4 + 1
+    mixed = (v(m), v(m + 1), (v(m) + NF // 2) % NF)
+    alike = (v(c), v(c + NF - 1), v(c + 1))
+    if isinstance(t, int):
+        return mixed if t < NF // 2 else alike
+    return tuple(jnp.where(t < NF // 2, x, y) for x, y in zip(mixed, alike))
+
+
 class Part:
-    def __init__(self, first, last, inner, leads):
-        self.first, self.last, self.inner, self.leads = first, last, inner, leads
-        pairs = sum(NF // 2 if 2 * d == NF else NF for d in range(first, last + 1))
-        self.pairs = -(-pairs // 8) * 8
+    def __init__(self, runs, inner, leads):
+        self.runs, self.inner, self.leads = runs, inner, leads
+        doubles = [double(t) for double, count in runs for t in range(count)]
+        self.blocks = [(a, b) for a, *both in doubles for b in both]
+        self.pairs = len(self.blocks)
         self.diagonal = 9 * self.pairs
         self.used = self.diagonal + len(inner) * DIAG_UP
         self.slot = self.diagonal + NF if inner else self.used
         self.trace = self.slot + 1
-        self.words = -(-(self.used + 2 * leads) // LANES) * LANES
-
-
-LEAD = Part(1, 4, (), True)
-REST = Part(5, 10, UPPER, False)
+        self.words = -(-(self.used + (0 if inner else 2)) // LANES) * LANES
+
+
+LEAD = Part(((near_pairs(1), 2 * NF),), (), True)
+REST = Part(((near_pairs(5), 2 * NF), (far_pairs, 16)), UPPER, False)
+assert {frozenset(pair) for part in (LEAD, REST) for pair in part.blocks} == {
+    frozenset((a, b)) for b in range(NF) for a in range(b)
+}
 
 
 def split(value):
@@ -51,16 +75,21 @@
     return dot(onehot, high) + dot(onehot, low)
 
 
-def fold(parts):
-    row = lax.broadcasted_iota(jnp.int32, parts[0].shape, 0)
-    for bit in (1, 2, 4):
-        keep = (row & bit) == 0
-        parts = [
-            jnp.where(keep, first, second)
-            + pltpu.roll(jnp.where(keep, second, first), 8 - bit, 0)
-            for first, second in zip(parts[0::2], parts[1::2])
-        ]
-    return parts[0]
+def merge(left, right, bit):
+    keep = (lax.broadcasted_iota(jnp.int32, next(iter(left.values())).shape, 0) & bit) == 0
+    return {
+        key: jnp.where(keep, one, right[key])
+        + pltpu.roll(jnp.where(keep, right[key], one), 8 - bit, 0)
+        for key, one in left.items()
+    }
+
+
+def octet(two):
+    halves = []
+    for half in range(2):
+        quarters = [merge(*two(2 * half + quarter), 1) for quarter in range(2)]
+        halves.append(merge(*quarters, 2))
+    return merge(*halves, 4)
 
 
 def lead_elements(plane, ndevices, capacity, *refs):
@@ -86,7 +115,7 @@
     large = [
         pltpu.make_async_copy(
             g_hbm.at[pl.ds(n * stripe, stripe)],
-            g_ref.at[pl.ds(n * stripe, stripe)],
+            g_ref.at[pl.ds(n * stripe, stripe), pl.ds(0, points)],
             sems.at[len(small) + n],
         )
         for n in range(STRIPES)
@@ -111,8 +140,7 @@
 
     place_ref[...] = place(owners)
     me = lax.axis_index("row") * lax.axis_size("col") + lax.axis_index("col")
-    ahead = owners // plane - me // plane
-    ahead = jnp.where(ahead < 0, ahead + ndevices // plane, ahead)
+    ahead = (owners // plane) ^ (me // plane)
     aside = owners % plane - me % plane
     aside = jnp.where(aside < 0, aside + plane, aside)
     where = place(ahead * plane + aside)
@@ -121,9 +149,9 @@
     weff = jnp.where(qrow < counts_ref[...] * GP, w_ref[...], 0.0)
 
     def weigh(m, inside):
-        g = g_ref[m]
+        g = g_ref[m, :points]
         weighted = g * weff
-        wg_ref[m] = weighted
+        wg_ref[m, :points] = weighted
         return inside + jnp.sum((weighted * g).reshape(points // 8, 8, count), axis=0)
 
     inside = jnp.zeros((8, count), jnp.float32)
@@ -147,11 +175,23 @@
             out_ref[:, words] = moved[k * rows : (k + 1) * rows]
 
 
-def rest_elements(g_ref, wg_ref, lines_ref, place_ref, out_ref, k_ref):
-    lam, mu, slots = (jnp.broadcast_to(lines_ref[n : n + 1, :], (8, k_ref.shape[1])) for n in range(3))
+def rest_elements(g_ref, wg_ref, lines_ref, place_ref, out_hbm, k_ref, out_ref, sems):
+    lam, mu, slots = (
+        jnp.broadcast_to(lines_ref[n : n + 1, :], (8, k_ref.shape[1])) for n in range(3)
+    )
     blocks(REST, g_ref, wg_ref, lam, mu, slots[:1], k_ref)
+    copies = []
     for words, moved in selected(REST, place_ref[...], out_ref.shape[0], k_ref):
         out_ref[:, words] = moved
+        n = len(copies)
+        if words.stop % (2 * LANES) == 0 or words.stop == REST.words:
+            done = pl.ds(n * 2 * LANES, words.stop - n * 2 * LANES)
+            copies.append(
+                pltpu.make_async_copy(out_ref.at[:, done], out_hbm.at[:, done], sems.at[n])
+            )
+            copies[-1].start()
+    for copy in copies:
+        copy.wait()
 
 
 def selected(part, where, width, k_ref):
@@ -164,47 +204,47 @@
 
 
 def blocks(part, g_ref, wg_ref, lam, mu, slots, k_ref):
-    points, count = g_ref.shape[1:]
+    points, count = g_ref.shape[1] - 8, g_ref.shape[2]
     both = lam + mu
 
-    def products(a, b, wanted):
-        sums = {}
+    def products(a, seconds, wanted):
+        sums = [{} for _ in seconds]
         for t in range(points // 8):
             rows = pl.ds(8 * t, 8)
             left = [wg_ref[3 * a + i, rows, :] for i in range(3)]
-            right = [g_ref[3 * b + j, rows, :] for j in range(3)]
-            for i, j in wanted:
-                term = left[i] * right[j]
-                sums[i, j] = term if t == 0 else sums[i, j] + term
+            for one, b in zip(sums, seconds):
+                right = [g_ref[3 * b + j, rows, :] for j in range(3)]
+                for i, j in wanted:
+                    term = left[i] * right[j]
+                    one[i, j] = term if t == 0 else one[i, j] + term
         return sums
 
-    def off_diagonal(group, carry):
-        sums = []
-        for k in range(8):
-            p = group * 8 + k
-            d = p // NF
-            a = p - d * NF
-            b = a + d + part.first
-            b = jnp.where(b >= NF, b - NF, b)
-            sums.append(products(a, b, FULL))
-        m = {ij: fold([one[ij] for one in sums]) for ij in FULL}
+    first = 0
+    for double, doubles in part.runs:
+
+        def off_diagonal(group, carry, double=double, first=first):
+            def two(k):
+                a, *seconds = double(group * 4 + k)
+                return products(a, seconds, FULL)
+
+            m = octet(two)
+            across = mu * (m[0, 0] + m[1, 1] + m[2, 2])
+            for i, j in FULL:
+                value = both * m[i, i] + across if i == j else lam * m[i, j] + mu * m[j, i]
+                start = pl.multiple_of((3 * i + j) * part.pairs + first + group * 8, 8)
+                k_ref[pl.ds(start, 8), :] = value
+            return carry
+
+        lax.fori_loop(0, doubles // 4, off_diagonal, 0)
+        first += 2 * doubles
+
+    def diagonal(group, carry):
+        def two(k):
+            own = [jnp.minimum(group * 8 + 2 * k + n, NF - 1) for n in range(2)]
+            return [products(a, [a], part.inner)[0] for a in own]
+
+        m = octet(two)
         across = mu * (m[0, 0] + m[1, 1] + m[2, 2])
-        for i, j in FULL:
-            value = both * m[i, i] + across if i == j else lam * m[i, j] + mu * m[j, i]
-            start = pl.multiple_of((3 * i + j) * part.pairs + group * 8, 8)
-            k_ref[pl.ds(start, 8), :] = value
-        return carry
-
-    lax.fori_loop(0, part.pairs // 8, off_diagonal, 0)
-
-    def diagonal(group, carry):
-        sums = []
-        for k in range(8):
-            a = jnp.minimum(group * 8 + k, NF - 1)
-            sums.append(products(a, a, part.inner))
-        m = {ij: fold([one[ij] for one in sums]) for ij in part.inner}
-        if (0, 0) in part.inner:
-            across = mu * (m[0, 0] + m[1, 1] + m[2, 2])
         for c, (i, j) in enumerate(part.inner):
             value = both * m[i, j] + across if i == j else both * m[i, j]
             start = pl.multiple_of(part.diagonal + c * DIAG_UP + group * 8, 8)
@@ -242,50 +282,56 @@
             out_ref[k * capacity : (k + 1) * capacity] = in_ref[l * capacity : (l + 1) * capacity]
 
 
-def lead_kernel(part, capacity, elements, *refs):
-    in_refs, (sum_ref, inverse_ref, all_ref) = refs[:-3], refs[-3:]
+def unfold(part, ref, whole_ref, after=lambda a: None):
+    entries = {}
+    for p, (a, b) in enumerate(part.blocks):
+        for i, j in FULL:
+            word = (3 * i + j) * part.pairs + p
+            entries.setdefault(3 * a + i, {})[3 * b + j] = word
+            entries.setdefault(3 * b + j, {})[3 * a + i] = word
+    for c, (i, j) in enumerate(part.inner):
+        for a in range(NF):
+            word = part.diagonal + c * DIAG_UP + a
+            entries[3 * a + i][3 * a + j] = entries[3 * a + j][3 * a + i] = word
+    for m in range(NDOF):
+        for n, word in sorted(entries[m].items()):
+            whole_ref[m, n, :] = ref[word, :]
+        if m % 3 == 2:
+            after(m // 3)
+
+
+def lead_owners(capacity, elements, *refs):
+    in_refs, (whole_ref, inverse_ref, all_ref, sum_ref) = refs[:-4], refs[-4:]
     rows = in_refs[0].shape[0]
     for l, in_ref in enumerate(in_refs):
         all_ref[l * rows : (l + 1) * rows] = in_ref[...]
-    total = jnp.sum(all_ref[:, part.trace : part.trace + 1]) / capacity
+    total = jnp.sum(all_ref[:, LEAD.trace : LEAD.trace + 1]) / capacity
     inverse = 1.0 / jnp.broadcast_to(total / (NDOF * elements), (SLOTS_DEV, LANES))
     inverse_ref[...] = inverse
-    gather_words(part, inverse, all_ref, sum_ref)
-
-
-def last_kernel(in_ref, inverse_ref, lead_ref, out_ref, sum_ref, whole_ref, sems):
+    gather_words(LEAD, inverse, all_ref, sum_ref)
+    unfold(LEAD, sum_ref, whole_ref)
+
+
+def rest_owners(in_ref, inverse_ref, whole_in, out_ref, whole_ref, sum_ref, sems):
+    del whole_in
     gather_words(REST, inverse_ref[...], in_ref, sum_ref)
-    sums = {LEAD: lead_ref, REST: sum_ref}
 
     def copy(stripe):
         rows = pl.ds(stripe * (NDOF // STRIPES), NDOF // STRIPES)
         return pltpu.make_async_copy(whole_ref.at[rows], out_ref.at[rows], sems.at[stripe])
 
-    for a in range(NF):
-        forth = NF // 2 if a < NF // 2 else NF // 2 - 1
-        back = NF - 1 - forth
-        for i in range(3):
-            m = 3 * a + i
-            for j in range(3):
-                for one, ref in sums.items():
-                    for d in range(one.first, one.last + 1):
-                        start = (d - one.first) * NF
-                        if d <= forth:
-                            b = (a + d) % NF
-                            word = (3 * i + j) * one.pairs + start + a
-                            whole_ref[m, 3 * b + j, :] = ref[word, :]
-                        if d <= back:
-                            b = (a - d) % NF
-                            word = (3 * j + i) * one.pairs + start + b
-                            whole_ref[m, 3 * b + j, :] = ref[word, :]
-                    ij = (min(i, j), max(i, j))
-                    if ij in one.inner:
-                        word = one.diagonal + one.inner.index(ij) * DIAG_UP + a
-                        whole_ref[m, 3 * a + j, :] = ref[word, :]
+    def after(a):
         if (a + 1) * STRIPES % NF == 0:
             copy((a + 1) * STRIPES // NF - 1).start()
+
+    unfold(REST, sum_ref, whole_ref, after)
     for stripe in range(STRIPES):
         copy(stripe).wait()
+
+
+def planes_of(nrow):
+    most = nrow & -nrow
+    return max(1, most // 2)
 
 
 def shards(grads, weights, counts, lame_first, shear, dest_owner, dest_slot):
@@ -294,16 +340,16 @@
     ndevices = nrow * ncol
     capacity = max(2, 2 * count // ndevices)
     width = ndevices * capacity
-    planes = nrow // 2 if nrow % 2 == 0 else nrow
+    planes = planes_of(nrow)
     plane = ndevices // planes
     f32 = lambda *shape: jax.ShapeDtypeStruct(shape, jnp.float32)
     line = lambda v: v.reshape(1, count)
     params = pltpu.CompilerParams(vmem_limit_bytes=20 * 2**20)
     vmem = pltpu.VMEM
     hbm = pl.BlockSpec(memory_space=pltpu.MemorySpace.HBM)
-    large = (NDOF, points, count)
-
-    near = lambda d, k: (d + k * plane) % ndevices
+    large = (NDOF, points + 8, count)
+
+    near = lambda d, k: (d // plane ^ k) * plane + d % plane
     beside = lambda d, l: d // plane * plane + (d + l) % plane
     cost = lambda part: pl.CostEstimate(
         flops=60000 * part.words, bytes_accessed=4000000, transcendentals=0
@@ -330,7 +376,7 @@
         *(
             pltpu.with_memory_space_constraint(v, pltpu.MemorySpace.HBM)
             for v in (
-                jnp.transpose(grads, (1, 2, 0, 3)).reshape(large),
+                jnp.transpose(grads, (1, 2, 0, 3)).reshape(NDOF, points, count),
                 weights,
                 line(counts),
                 line(lame_first),
@@ -340,13 +386,18 @@
             )
         )
     )
-    for k in range(1, planes):
+    for k in HOPS(planes):
         pairs = [(d, near(d, k)) for d in range(ndevices)]
         blocks[k] = lax.ppermute(blocks[k], AXES, pairs)
     rest = pl.pallas_call(
         rest_elements,
         out_shape=f32(width, REST.words),
-        scratch_shapes=[vmem((REST.words, count), jnp.float32)],
+        out_specs=pl.BlockSpec(memory_space=pl.ANY),
+        scratch_shapes=[
+            vmem((REST.words, count), jnp.float32),
+            vmem((width, REST.words), jnp.float32),
+            pltpu.SemaphoreType.DMA((-(-REST.words // (2 * LANES)),)),
+        ],
         compiler_params=params,
         cost_estimate=cost(REST),
         name="elements_rest",
@@ -368,25 +419,29 @@
     for l in range(1, plane):
         pairs = [(d, beside(d, l)) for d in range(ndevices)]
         blocks[l] = lax.ppermute(blocks[l], AXES, pairs)
+    whole = f32(NDOF, NDOF, SLOTS_DEV)
     lead, inverse = pl.pallas_call(
-        functools.partial(lead_kernel, LEAD, capacity, count * ndevices),
-        out_shape=[f32(LEAD.words, SLOTS_DEV), f32(SLOTS_DEV, LANES)],
-        scratch_shapes=[pltpu.VMEM((width, LEAD.words), jnp.float32)],
+        functools.partial(lead_owners, capacity, count * ndevices),
+        out_shape=[whole, f32(SLOTS_DEV, LANES)],
+        scratch_shapes=[
+            vmem((width, LEAD.words), jnp.float32),
+            vmem((LEAD.words, SLOTS_DEV), jnp.float32),
+        ],
         compiler_params=params,
         name="owners_lead",
     )(*blocks)
     return pl.pallas_call(
-        last_kernel,
-        out_shape=f32(NDOF, NDOF, SLOTS_DEV),
-        out_specs=pl.BlockSpec(memory_space=pl.ANY),
+        rest_owners,
+        out_shape=[whole, whole],
+        out_specs=[pl.BlockSpec(memory_space=pl.ANY), pl.BlockSpec(memory_space=pltpu.VMEM)],
+        input_output_aliases={2: 1},
         scratch_shapes=[
-            pltpu.VMEM((REST.words, SLOTS_DEV), jnp.float32),
-            pltpu.VMEM((NDOF, NDOF, SLOTS_DEV), jnp.float32),
+            vmem((REST.words, SLOTS_DEV), jnp.float32),
             pltpu.SemaphoreType.DMA((STRIPES,)),
         ],
         compiler_params=params,
-        name="owners_last",
-    )(rest, inverse, lead)
+        name="owners_rest",
+    )(rest, inverse, lead)[0]
 
 
 def solution(mesh):

time: 79.2 us -> 77.1 us (0.973)
  Pallas kernels: 15.3 us -> 13.2 us
  waiting for transfers between devices: 46.7 us -> 47.7 us
  starting transfers between devices: 16.9 us -> 16 us
    pallas_call x3, Pallas kernels: 9.66 us -> 8.33 us  [the longest x1 5.42 us: shards(): pl.pallas_call(rest_elements, out_shape=f32(width, REST.words), out_specs...]
    ppermute x3, waiting for transfers between devices: 40.5 us -> 41.4 us  [shards(): blocks[k] = lax.ppermute(blocks[k], AXES, pairs)]
    ppermute x3, starting transfers between devices: 3.67 us -> 2.71 us  [shards(): blocks[k] = lax.ppermute(blocks[k], AXES, pairs)]
    pallas_call x1, Pallas kernels: 5.59 us -> 4.78 us  [shards(): pl.pallas_call(functools.partial(lead_elements, plane, ndevices, capacity...]
where the time goes in v3:
time: 77.1 us; the launch traced here: 76.9 us
  waiting for transfers between devices  47.7 us (62%)
  starting transfers between devices  16 us (21%)
  Pallas kernels  13.2 us (17%)
    ppermute x3, waiting for transfers between devices, shards(): blocks[k] = lax.ppermute(blocks[k], AXES, pairs)  41.4 us
    ppermute x7, starting transfers between devices, shards(): blocks[l] = lax.ppermute(blocks[l], AXES, pairs)  6.96 us
    all_to_all x1, starting transfers between devices, shards(): lax.all_to_all(rest.reshape(ndevices, capacity, REST.words), AXES, split_...  6.31 us
    ppermute x7, waiting for transfers between devices, shards(): blocks[l] = lax.ppermute(blocks[l], AXES, pairs)  6.28 us
    pallas_call x1, Pallas kernels, shards(): pl.pallas_call(rest_elements, out_shape=f32(width, REST.words), out_specs...  5.42 us
    pallas_call x1, Pallas kernels, shards(): pl.pallas_call(functools.partial(lead_elements, plane, ndevices, capacity...  4.78 us
    ppermute x3, starting transfers between devices, shards(): blocks[k] = lax.ppermute(blocks[k], AXES, pairs)  2.71 us
    pallas_call x1, Pallas kernels, shards(): pl.pallas_call(rest_owners, out_shape=[whole, whole], out_specs=[pl.Block...  2.11 us
  transfers between devices with their start and end apart: 11, of which 5 were waited for; matrix products, arithmetic and copies ran while one was open for 0% of the time, Pallas kernels for 1%

profile of v3, /device:TPU:11, one launch (start us, length us, event | category | flops | bytes accessed | tf_op | source)
XLA Modules:
  0.0 76.9 jit_solution(9609427658823370881)
XLA Ops:
  0.0 4.8 %elements_lead.1 = (f32[64,768]{1,0:T(8,128)S(1)}, f32[64,768]{1,0:T(8,128)S(1)}, f32[64,768]{1,0:T(8,128)S(1)}, f32[64,768]{1,0:T(8,128)S(1)}, s32[1,128]{1,0:T...) custom-call(f32[60,64,128]{2,1,0:T(8,128)} %bitcast.11, ...), custom_call_target="tpu_custom_call" | custom-call | flops 46080000 | bytes 4000000 | tf_op jit(solution)/shard_map/elements_lead/pallas_call | solution.py:357
  4.8 5.4 %elements_rest.1 = f32[256,1152]{1,0:T(8,128)} custom-call(f32[60,72,128]{2,1,0:T(8,128)S(1)} %get-tuple-element.24.g_ref, f32[60,72,128]{2,1,0:T(8,128)S(1)} %get-tuple-element.25.wg_ref, f32[8,128]{1,0:T(8,128)S(1)} %get-tuple-element.26.lines_ref, s32[1,128]{1,0:T(1,128)S(1)} %get-tuple-element.27.place_ref), custom_call_target="tpu_custom_call" | custom-call | flops 69120000 | bytes 4000000 | tf_op jit(solution)/shard_map/elements_rest/pallas_call | solution.py:392
  10.2 6.3 %all-to-all-start = ((f32[32,8,1152]{2,1,0:T(8,128)}), f32[32,8,1152]{2,1,0:T(8,128)S(1)}, u32[]{:S(2)}, u32[]{:S(2)}) async-start(f32[32,8,1152]{2,1,0:T(8,128)} %bitcast.7), calls=%async_computation | async-start | bytes 2359296 | tf_op jit(solution)/shard_map/all_to_all | solution.py:405
  16.5 0.3 collective-permute-start
  16.9 2.1 %collective-permute-start.1 = (f32[64,768]{1,0:T(8,128)S(1)}, f32[64,768]{1,0:T(8,128)S(1)}, u32[]{:S(2)}, u32[]{:S(2)}) collective-permute-start(f32[64,768]{1,0:T(8,128)S(1)} %get-tuple-element.30), channel_id=1, source_target_pairs={{0,16},{1,17},{2,18},{3,19},{4,20},{5,21},{6,22},{7,23},{8,24},{9,... | collective-permute-start | bytes 589832 | tf_op jit(solution)/shard_map/ppermute | solution.py:391
  19.0 0.3 collective-permute-start.2
  19.2 21.5 %collective-permute-done.refs_1_ = f32[64,768]{1,0:T(8,128)S(1)} collective-permute-done((f32[64,768]{1,0:T(8,128)S(1)}, f32[64,768]{1,0:T(8,128)S(1)}, u32[]{:S(2)}, u32[]{:S(2)}) %collective-permute-start) | collective-permute-done | bytes 196640 | tf_op jit(solution)/shard_map/ppermute | solution.py:391
  40.7 13.8 %collective-permute-done.1.refs_2_ = f32[64,768]{1,0:T(8,128)S(1)} collective-permute-done((f32[64,768]{1,0:T(8,128)S(1)}, f32[64,768]{1,0:T(8,128)S(1)}, u32[]{:S(2)}, u32[]{:S(2)}) %collective-permute-start.1) | collective-permute-done | bytes 196640 | tf_op jit(solution)/shard_map/ppermute | solution.py:391
  54.6 6.1 %collective-permute-done.2.refs_3_ = f32[64,768]{1,0:T(8,128)S(1)} collective-permute-done((f32[64,768]{1,0:T(8,128)S(1)}, f32[64,768]{1,0:T(8,128)S(1)}, u32[]{:S(2)}, u32[]{:S(2)}) %collective-permute-start.2) | collective-permute-done | bytes 196640 | tf_op jit(solution)/shard_map/ppermute | solution.py:391
  60.7 0.1 relay.1
  60.7 2.1 %collective-permute-start.3 = (f32[32,768]{1,0:T(8,128)S(1)}, f32[32,768]{1,0:T(8,128)S(1)}, u32[]{:S(2)}, u32[]{:S(2)}) collective-permute-start(f32[32,768]{1,0:T(8,128)S(1)} %get-tuple-element.33), channel_id=1, source_target_pairs={{0,1},{1,2},{2,3},{3,4},{4,5},{5,6},{6,7},{7,0},{8,9},{9,10},{10,1... | collective-permute-start | bytes 294920 | tf_op jit(solution)/shard_map/ppermute | solution.py:421
  62.8 1.2 %collective-permute-start.4 = (f32[32,768]{1,0:T(8,128)S(1)}, f32[32,768]{1,0:T(8,128)S(1)}, u32[]{:S(2)}, u32[]{:S(2)}) collective-permute-start(f32[32,768]{1,0:T(8,128)S(1)} %get-tuple-element.34), channel_id=1, source_target_pairs={{0,2},{1,3},{2,4},{3,5},{4,6},{5,7},{6,0},{7,1},{8,10},{9,11},{10,... | collective-permute-start | bytes 294920 | tf_op jit(solution)/shard_map/ppermute | solution.py:421
  64.0 0.0 collective-permute-start.5
  64.0 0.6 collective-permute-start.6
  64.6 1.7 %collective-permute-start.7 = (f32[32,768]{1,0:T(8,128)S(1)}, f32[32,768]{1,0:T(8,128)S(1)}, u32[]{:S(2)}, u32[]{:S(2)}) collective-permute-start(f32[32,768]{1,0:T(8,128)S(1)} %get-tuple-element.37), channel_id=1, source_target_pairs={{0,5},{1,6},{2,7},{3,0},{4,1},{5,2},{6,3},{7,4},{8,13},{9,14},{10,... | collective-permute-start | bytes 294920 | tf_op jit(solution)/shard_map/ppermute | solution.py:421
  66.3 0.0 collective-permute-done.3.refs_1_
  66.3 1.1 %collective-permute-start.8 = (f32[32,768]{1,0:T(8,128)S(1)}, f32[32,768]{1,0:T(8,128)S(1)}, u32[]{:S(2)}, u32[]{:S(2)}) collective-permute-start(f32[32,768]{1,0:T(8,128)S(1)} %get-tuple-element.38), channel_id=1, source_target_pairs={{0,6},{1,7},{2,0},{3,1},{4,2},{5,3},{6,4},{7,5},{8,14},{9,15},{10,... | collective-permute-start | bytes 294920 | tf_op jit(solution)/shard_map/ppermute | solution.py:421
  67.4 0.0 collective-permute-done.4.refs_2_
  67.4 0.3 collective-permute-start.9
  67.7 0.9 %collective-permute-done.5.refs_3_ = f32[32,768]{1,0:T(8,128)S(1)} collective-permute-done((f32[32,768]{1,0:T(8,128)S(1)}, f32[32,768]{1,0:T(8,128)S(1)}, u32[]{:S(2)}, u32[]{:S(2)}) %collective-permute-start.5) | collective-permute-done | bytes 98336 | tf_op jit(solution)/shard_map/ppermute | solution.py:421
  68.6 0.0 collective-permute-done.6.refs_4_
  68.6 5.4 %collective-permute-done.7.refs_5_ = f32[32,768]{1,0:T(8,128)S(1)} collective-permute-done((f32[32,768]{1,0:T(8,128)S(1)}, f32[32,768]{1,0:T(8,128)S(1)}, u32[]{:S(2)}, u32[]{:S(2)}) %collective-permute-start.7) | collective-permute-done | bytes 98336 | tf_op jit(solution)/shard_map/ppermute | solution.py:421
  74.0 0.0 collective-permute-done.8.refs_6_
  74.0 0.0 collective-permute-done.9.refs_7_
  74.0 0.8 %owners_lead.1 = (f32[60,60,128]{2,1,0:T(8,128)S(1)}, f32[128,128]{1,0:T(8,128)S(1)}) custom-call(f32[32,768]{1,0:T(8,128)S(1)} %get-tuple-element.32.refs_0_, f32[32,768]{1,0:T(8,128)S(1)} %collective-permute-done.3.refs_1_, f32[32,768]{1,0:T(8,128)S(1)} %collective-permute-done.4.refs_2_, f32[32,768]{1,0:T(8,128)S(1)} %collective-permute-done.5.refs_3_, ...), custom_call_target="tpu_custom_call" | custom-call | tf_op jit(solution)/shard_map/owners_lead/pallas_call | solution.py:423
  74.8 0.0 all-to-all-done
  74.8 2.1 %owners_rest.1 = (f32[60,60,128]{2,1,0:T(8,128)}, f32[60,60,128]{2,1,0:T(8,128)S(1)}) custom-call(f32[256,1152]{1,0:T(8,128)S(1)} %bitcast.10, f32[128,128]{1,0:T(8,128)S(1)} %get-tuple-element.40.inverse_ref, f32[60,60,128]{2,1,0:T(8,128)S(1)} %get-tuple-element.41.whole_in), custom_call_target="tpu_custom_call", output_to_operand_aliasing={{1}: (2, {})} | custom-call | tf_op jit(solution)/shard_map/owners_rest/pallas_call | solution.py:433
Async XLA Ops:
  10.2 64.6 %all-to-all-start = ((f32[32,8,1152]{2,1,0:T(8,128)}), f32[32,8,1152]{2,1,0:T(8,128)S(1)}, u32[]{:S(2)}, u32[]{:S(2)}) async-start(f32[32,8,1152]{2,1,0:T(8,128)} %bitcast.7), calls=%async_computation | async-start | bytes 2359296 | tf_op jit(solution)/shard_map/all_to_all | solution.py:405
  16.5 24.2 %collective-permute-start = (f32[64,768]{1,0:T(8,128)S(1)}, f32[64,768]{1,0:T(8,128)S(1)}, u32[]{:S(2)}, u32[]{:S(2)}) collective-permute-start(f32[64,768]{1,0:T(8,128)S(1)} %get-tuple-element.29), channel_id=1, source_target_pairs={{0,8},{1,9},{2,10},{3,11},{4,12},{5,13},{6,14},{7,15},{8,0},{9,1},... | collective-permute-start | bytes 589832 | tf_op jit(solution)/shard_map/ppermute | solution.py:391
  16.9 37.7 %collective-permute-start.1 = (f32[64,768]{1,0:T(8,128)S(1)}, f32[64,768]{1,0:T(8,128)S(1)}, u32[]{:S(2)}, u32[]{:S(2)}) collective-permute-start(f32[64,768]{1,0:T(8,128)S(1)} %get-tuple-element.30), channel_id=1, source_target_pairs={{0,16},{1,17},{2,18},{3,19},{4,20},{5,21},{6,22},{7,23},{8,24},{9,... | collective-permute-start | bytes 589832 | tf_op jit(solution)/shard_map/ppermute | solution.py:391
  19.0 41.7 %collective-permute-start.2 = (f32[64,768]{1,0:T(8,128)S(1)}, f32[64,768]{1,0:T(8,128)S(1)}, u32[]{:S(2)}, u32[]{:S(2)}) collective-permute-start(f32[64,768]{1,0:T(8,128)S(1)} %get-tuple-element.31), channel_id=1, source_target_pairs={{0,24},{1,25},{2,26},{3,27},{4,28},{5,29},{6,30},{7,31},{8,16},{9,... | collective-permute-start | bytes 589832 | tf_op jit(solution)/shard_map/ppermute | solution.py:391
  60.7 5.6 %collective-permute-start.3 = (f32[32,768]{1,0:T(8,128)S(1)}, f32[32,768]{1,0:T(8,128)S(1)}, u32[]{:S(2)}, u32[]{:S(2)}) collective-permute-start(f32[32,768]{1,0:T(8,128)S(1)} %get-tuple-element.33), channel_id=1, source_target_pairs={{0,1},{1,2},{2,3},{3,4},{4,5},{5,6},{6,7},{7,0},{8,9},{9,10},{10,1... | collective-permute-start | bytes 294920 | tf_op jit(solution)/shard_map/ppermute | solution.py:421
  62.8 4.7 %collective-permute-start.4 = (f32[32,768]{1,0:T(8,128)S(1)}, f32[32,768]{1,0:T(8,128)S(1)}, u32[]{:S(2)}, u32[]{:S(2)}) collective-permute-start(f32[32,768]{1,0:T(8,128)S(1)} %get-tuple-element.34), channel_id=1, source_target_pairs={{0,2},{1,3},{2,4},{3,5},{4,6},{5,7},{6,0},{7,1},{8,10},{9,11},{10,... | collective-permute-start | bytes 294920 | tf_op jit(solution)/shard_map/ppermute | solution.py:421
  64.0 4.6 %collective-permute-start.5 = (f32[32,768]{1,0:T(8,128)S(1)}, f32[32,768]{1,0:T(8,128)S(1)}, u32[]{:S(2)}, u32[]{:S(2)}) collective-permute-start(f32[32,768]{1,0:T(8,128)S(1)} %get-tuple-element.35), channel_id=1, source_target_pairs={{0,3},{1,4},{2,5},{3,6},{4,7},{5,0},{6,1},{7,2},{8,11},{9,12},{10,... | collective-permute-start | bytes 294920 | tf_op jit(solution)/shard_map/ppermute | solution.py:421
  64.0 4.6 %collective-permute-start.6 = (f32[32,768]{1,0:T(8,128)S(1)}, f32[32,768]{1,0:T(8,128)S(1)}, u32[]{:S(2)}, u32[]{:S(2)}) collective-permute-start(f32[32,768]{1,0:T(8,128)S(1)} %get-tuple-element.36), channel_id=1, source_target_pairs={{0,4},{1,5},{2,6},{3,7},{4,0},{5,1},{6,2},{7,3},{8,12},{9,13},{10,... | collective-permute-start | bytes 294920 | tf_op jit(solution)/shard_map/ppermute | solution.py:421
  64.6 9.4 %collective-permute-start.7 = (f32[32,768]{1,0:T(8,128)S(1)}, f32[32,768]{1,0:T(8,128)S(1)}, u32[]{:S(2)}, u32[]{:S(2)}) collective-permute-start(f32[32,768]{1,0:T(8,128)S(1)} %get-tuple-element.37), channel_id=1, source_target_pairs={{0,5},{1,6},{2,7},{3,0},{4,1},{5,2},{6,3},{7,4},{8,13},{9,14},{10,... | collective-permute-start | bytes 294920 | tf_op jit(solution)/shard_map/ppermute | solution.py:421
  66.3 7.7 %collective-permute-start.8 = (f32[32,768]{1,0:T(8,128)S(1)}, f32[32,768]{1,0:T(8,128)S(1)}, u32[]{:S(2)}, u32[]{:S(2)}) collective-permute-start(f32[32,768]{1,0:T(8,128)S(1)} %get-tuple-element.38), channel_id=1, source_target_pairs={{0,6},{1,7},{2,0},{3,1},{4,2},{5,3},{6,4},{7,5},{8,14},{9,15},{10,... | collective-permute-start | bytes 294920 | tf_op jit(solution)/shard_map/ppermute | solution.py:421
  67.4 6.5 %collective-permute-start.9 = (f32[32,768]{1,0:T(8,128)S(1)}, f32[32,768]{1,0:T(8,128)S(1)}, u32[]{:S(2)}, u32[]{:S(2)}) collective-permute-start(f32[32,768]{1,0:T(8,128)S(1)} %get-tuple-element.39), channel_id=1, source_target_pairs={{0,7},{1,0},{2,1},{3,2},{4,3},{5,4},{6,5},{7,6},{8,15},{9,8},{10,9... | collective-permute-start | bytes 294920 | tf_op jit(solution)/shard_map/ppermute | solution.py:421
